TPU v7x, 32 devices: a whole 2x2x4 slice. The times are simulated.
32 devices in a mesh: dp: 16 (over z, y, core), space: 2 (over x).
Axes of the slice: x: 2, y: 2, z: 4, core: 2. Of those that a mesh axis runs over, the one named last changes fastest.
Arguments:
- images: bfloat16 [16, 3, 512, 512], P('dp', None, 'space'), may hold values from -6 to 6
- pos_embed: bfloat16 [1024, 1280], P('space'), may hold values from -3 to 3
- conv_first: bfloat16 [3, 3, 3, 64], replicated, may hold values from -1.75 to 1.75
- conv_second: bfloat16 [3, 3, 64, 128], replicated, may hold values from -0.375 to 0.375
- conv_third: bfloat16 [3, 3, 128, 256], replicated, may hold values from -0.25 to 0.25
- conv_fourth: bfloat16 [3, 3, 256, 512], replicated, may hold values from -0.1875 to 0.1875
- proj_weight: bfloat16 [512, 1280], replicated, may hold values from -0.375 to 0.375
- ln_first: float32 [1280], replicated, may hold values from 0.25 to 1.75
- qkv_weight: bfloat16 [1280, 3, 1280], P('dp', None, 'space'), as said below
- out_weight: bfloat16 [1280, 1280], P('space', 'dp'), may hold values from -0.15625 to 0.15625
- ln_second: float32 [1280], replicated, may hold values from 0.25 to 1.75
- up_weight: bfloat16 [1280, 5120], P('dp', 'space'), may hold values from -0.15625 to 0.15625
- down_weight: bfloat16 [5120, 1280], P('space', 'dp'), may hold values from -0.125 to 0.125
Outputs:
- encoded: bfloat16 [16, 1024, 1280], P('dp', 'space')
Inputs may be any that keep to these rules, and one draw needn't show every extreme that they name: `qkv_weight`: every entry is at most 135 * 1280 ** -0.5 in magnitude.
All inputs are finite; a program needn't handle non-finite values.
Results may differ from a plain program's by a relative error of at most 0.014.
Values may be sent and summed in bfloat16 or wider, within the bound.
A program may use at most 128 MiB of HBM per device.

v0:
```python
import jax
import jax.numpy as jnp
from jax import lax
from jax.sharding import PartitionSpec as P

HEADS = 16


def passed_along(value, axis, steps):
    count = lax.axis_size(axis)
    leading, last = (max(0, -steps), min(count, count - steps))
    return lax.ppermute(value, axis, [(source, source + steps) for source in range(leading, last)])


def conv_rows(image_field, kernel, spec):
    out = lax.conv_general_dilated(
        image_field,
        kernel,
        (2, 2),
        ((0, 0), (1, 1)),
        dimension_numbers=spec,
        preferred_element_type=jnp.float32,
    )
    return jax.nn.relu(out).astype(jnp.bfloat16)


def layer_norm(values, gain):
    wide = values.astype(jnp.float32)
    center = wide - jnp.mean(wide, axis=-1, keepdims=True)
    spread = jnp.mean(center * center, axis=-1, keepdims=True)
    return (center * lax.rsqrt(spread + 1e-06) * gain).astype(jnp.bfloat16)


def attend(query, keys, values):
    head_size = query.shape[-1]
    divisor = jnp.sqrt(jnp.float32(head_size))

    def one_head(items):
        head_query, head_keys, head_values = items
        scores = (
            jnp.einsum("gqd,gkd->gqk", head_query, head_keys, preferred_element_type=jnp.float32)
            / divisor
        )
        weights = jax.nn.softmax(scores, axis=-1).astype(jnp.bfloat16)
        return jnp.einsum(
            "gqk,gkd->gqd", weights, head_values, preferred_element_type=jnp.float32
        ).astype(jnp.bfloat16)

    mixed = lax.map(
        one_head, (jnp.moveaxis(query, 2, 0), jnp.moveaxis(keys, 2, 0), jnp.moveaxis(values, 2, 0))
    )
    return jnp.moveaxis(mixed, 0, 2)


def device_rows(values, start, total, groups, per_device, weight):
    token_start = start // groups
    token_count = total // groups
    slab = lax.dynamic_slice_in_dim(values, token_start, token_count, 1)
    owners = token_count // per_device
    slab = slab.reshape(groups, owners, per_device, values.shape[2])
    slab = jnp.transpose(slab, (1, 0, 2, 3)).reshape(total, values.shape[2])
    return jnp.dot(slab, weight, preferred_element_type=jnp.float32)


def on_device(
    images,
    pos_embed,
    conv_first,
    conv_second,
    conv_third,
    conv_fourth,
    proj_weight,
    ln_first,
    qkv_weight,
    out_weight,
    ln_second,
    up_weight,
    down_weight,
):
    spec_first = ("NCHW", "HWIO", "NHWC")
    spec_later = ("NHWC", "HWIO", "NHWC")
    margin = passed_along(images[:, :, -15:, :], "space", 1)
    stem_out = conv_rows(jnp.concatenate([margin, images], axis=2), conv_first, spec_first)
    for kernel in (conv_second, conv_third, conv_fourth):
        stem_out = conv_rows(stem_out, kernel, spec_later)
    groups, height, across, channels = stem_out.shape
    flat = stem_out.reshape(groups, height * across, channels)
    tokens = (
        jnp.dot(flat, proj_weight, preferred_element_type=jnp.float32)
        + pos_embed.astype(jnp.float32)
    ).astype(jnp.bfloat16)
    qkv_part, out_part = (
        lax.all_gather(qkv_weight, "dp", axis=0, tiled=True),
        lax.all_gather(out_weight, "dp", axis=1, tiled=True),
    )
    width = tokens.shape[2]
    count = tokens.shape[1]
    local = qkv_part.shape[2]
    head_size = width // HEADS
    local_heads = local // head_size
    qkv_matrix = qkv_part.reshape(width, 3 * local)
    qkv_all = jnp.dot(
        layer_norm(lax.all_gather(tokens, "space", axis=1, tiled=True), ln_first),
        qkv_matrix,
        preferred_element_type=jnp.float32,
    ).astype(jnp.bfloat16)
    seen = qkv_all.shape[1]
    qkv_all = qkv_all.reshape(groups, seen, 3, local_heads, head_size)
    mixed = attend(qkv_all[:, :, 0], qkv_all[:, :, 1], qkv_all[:, :, 2]).reshape(
        groups, seen, local
    )
    attn_sum = (
        lax.psum_scatter(
            device_rows(
                mixed,
                jnp.int32(0),
                groups * count * lax.axis_size("space"),
                groups,
                count,
                out_part,
            ).astype(jnp.bfloat16),
            "space",
            scatter_dimension=0,
            tiled=True,
        )
        .astype(jnp.float32)
        .reshape(groups, count, width)
    )
    after_attn = (tokens.astype(jnp.float32) + attn_sum).astype(jnp.bfloat16)
    normed_two = layer_norm(after_attn, ln_second)
    group_rows = lax.all_gather(normed_two, "space", axis=1, tiled=True)
    seen_rows = group_rows.shape[1]
    hidden_cols = up_weight.shape[1]
    start_hidden = jnp.zeros((groups, seen_rows, hidden_cols), jnp.float32)
    before_gelu = start_hidden + jnp.einsum(
        "gtd,df->gtf",
        group_rows,
        lax.all_gather(up_weight, "dp", axis=0, tiled=True),
        preferred_element_type=jnp.float32,
    )
    hidden = jax.nn.gelu(before_gelu, approximate=False).astype(jnp.bfloat16)
    down_part = lax.all_gather(down_weight, "dp", axis=1, tiled=True)
    mlp_sum = (
        lax.psum_scatter(
            device_rows(
                hidden,
                jnp.int32(0),
                groups * count * lax.axis_size("space"),
                groups,
                count,
                down_part,
            ).astype(jnp.bfloat16),
            "space",
            scatter_dimension=0,
            tiled=True,
        )
        .astype(jnp.float32)
        .reshape(groups, count, width)
    )
    return (after_attn.astype(jnp.float32) + mlp_sum).astype(jnp.bfloat16)


def solution(mesh):
    placed = (
        P("dp", None, "space", None),
        P("space", None),
        P(),
        P(),
        P(),
        P(),
        P(),
        P(),
        P("dp", None, "space"),
        P("space", "dp"),
        P(),
        P("dp", "space"),
        P("space", "dp"),
    )
    return jax.shard_map(
        on_device, mesh=mesh, in_specs=placed, out_specs=P("dp", "space", None), check_vma=False
    )
```

profile of v0, /device:TPU:0, one launch (start us, length us, event | category | flops | bytes accessed | tf_op | source)
XLA Modules:
  0.0 586.7 jit_solution(12435895969867735964)
XLA Ops:
  7.5 4.9 collective-permute-start
  15.9 2.9 reshape.228
  18.8 19.6 %copy.46 = bf16[3,271,1,8,66]{3,0,4,1,2:T(4,128)(2,1)} copy(bf16[3,271,1,8,66]{4,3,1,0,2:T(8,128)(2,1)} %reshape.228) | data formatting | bytes 1717056 | tf_op jit(solution)/shard_map/conv_general_dilated | solution.py:16
  39.8 27.8 %fusion.44 = bf16[135,8,33,64]{3,1,2,0:T(8,128)(2,1)} fusion(pred[8,33]{0,1:T(8,128)(4,1)S(1)} %copy-done.8, bf16[3,3,3,64]{3,2,1,0:T(4,128)(2,1)S(1)} %copy-done.6, bf16[3,271,1,7,2]{3,0,4,1,2:T(4,128)(2,1)S(1)} %slice.25, bf16[3,271,1,8,66]{3,0,4,1,2:T(4,128)(2,1)} %copy.46), kind=kOutput, calls=%fused_computation.57 | convolution fusion | flops 134949312 | bytes 5446932 | tf_op jit(solution)/shard_map/conv_general_dilated | solution.py:16
  67.6 16.3 %copy.47 = bf16[135,8,33,64]{0,3,2,1:T(8,128)(2,1)} copy(bf16[135,8,33,64]{3,1,2,0:T(8,128)(2,1)} %fusion.44) | data formatting | bytes 9123840 | tf_op jit(solution)/shard_map/convert_element_type | solution.py:24
  84.0 8.3 %slice.26 = bf16[135,1,256,64]{0,3,2,1:T(8,128)(2,1)} slice(bf16[135,1,264,64]{0,3,2,1:T(8,128)(2,1)} %bitcast.122), slice={[0:135], [0:1], [0:256], [0:64]} | slice | bytes 8847360 | tf_op jit(solution)/shard_map/convert_element_type | solution.py:24
  92.3 15.6 %copy.48 = bf16[135,1,8,32,64]{4,2,3,0,1:T(8,128)(2,1)} copy(bf16[135,1,8,32,64]{0,4,3,2,1:T(8,128)(2,1)} %bitcast.123) | data formatting | bytes 8847360 | tf_op jit(solution)/shard_map/convert_element_type | solution.py:24
  109.1 6.6 %fusion.86 = bf16[67,1,8,16,128]{4,2,3,0,1:T(8,128)(2,1)S(1)} fusion(bf16[3,3,64,128]{3,2,1,0:T(8,128)(2,1)S(1)} %copy-done.5, bf16[135,1,7,1,64]{4,2,3,0,1:T(8,128)(2,1)S(1)} %get-tuple-element.63, bf16[135,1,7,1,64]{4,2,3,0,1:T(8,128)(2,1)S(1)} %get-tuple-element.62, bf16[135,1,8,32,64]{4,2,3,0,1:T(8,128)(2,1)} %copy.48), kind=kOutput, calls=%fused_computation.105 | convolution fusion | flops 1290278912 | bytes 7008512 | tf_op jit(solution)/shard_map/conv_general_dilated | solution.py:16
  119.3 3.7 fusion.63
  124.5 39.7 %all-gather.17.cloned.1.call-done = bf16[1024,1280]{1,0:T(8,128)(2,1)} async-done(((bf16[512,1280]{1,0:T(8,128)(2,1)}), bf16[1024,1280]{1,0:T(8,128)(2,1)}) %all-gather.17.cloned.1.call-update) | async-done | bytes 2621456 | tf_op jit(solution)/shard_map/all_gather | solution.py:103
  169.0 51.6 %all-gather.9.cloned.1.call-done = bf16[1280,3,640]{2,0,1:T(8,128)(2,1)} async-done(((bf16[80,3,640]{2,0,1:T(8,128)(2,1)}), bf16[1280,3,640]{2,0,1:T(8,128)(2,1)}) %all-gather.9.cloned.1.call-update) | async-done | bytes 4915216 | tf_op jit(solution)/shard_map/all_gather | solution.py:93
  220.6 8.2 %copy.52 = bf16[1280,3,640]{0,2,1:T(8,128)(2,1)} copy(bf16[1280,3,640]{2,0,1:T(8,128)(2,1)} %all-gather.9.cloned.1.call-done) | data formatting | bytes 9830400 | tf_op jit(solution)/shard_map/all_gather | solution.py:93
  228.8 10.3 %convolution_convert_fusion.1 = bf16[1024,1920]{1,0:T(8,128)(2,1)} fusion(bf16[1280,1920]{0,1:T(8,128)(2,1)} %bitcast.125, bf16[1024,1280]{1,0:T(8,128)(2,1)} %all-gather.17.cloned.1.call-done, f32[1280]{0:T(1024)S(1)} %copy-done.7, f32[1024]{0:T(1024)S(1)} %add_rsqrt_fusion, f32[1024]{0:T(1024)S(1)} %broadcast_multiply_fusion), kind=kOutput, calls=%fused_computation.78 | convolution fusion | flops 5041684480 | bytes 11482112 | tf_op jit(solution)/shard_map/dot_general | solution.py:102
  239.0 6.3 %copy.53 = bf16[1024,1920]{0,1:T(8,128)(2,1)} copy(bf16[1024,1920]{1,0:T(8,128)(2,1)} %convolution_convert_fusion.1) | data formatting | bytes 7864320 | tf_op jit(solution)/shard_map/convert_element_type | solution.py:106
  245.3 4.2 slice_bitcast_fusion
  249.5 39.8 %while.10 = (s32[]{:T(128)}, bf16[8,1,1024,80]{2,3,1,0:T(8,128)(2,1)}, bf16[8,1,1024,80]{2,3,0,1:T(8,128)(2,1)}, bf16[8,1,1024,80]{2,3,0,1:T(8,128)(2,1)S(1)}, bf16[8,1,1024,80]{2,3,0,1:T(8,128)(2,1)}, /*index=5*/s32[]{:T(128)}) while((s32[]{:T(128)}, bf16[8,1,1024,80]{2,3,1,0:T(8,128)(2,1)}, bf16[8,1,1024,80]{2,3,0,1:T(8,128)(2,1)}, ...), condition=%wide.region_5.6_spmd, body=%wide.region_2.5_spmd.sunk | while | flops 345061376 | bytes 13260869 | solution.py:49
  289.4 5.5 convolution_convert_fusion
  296.2 35.4 %reduce-scatter.3.cloned.1.call-done = bf16[512,1280]{1,0:T(8,128)(2,1)} async-done(((bf16[1024,1280]{1,0:T(8,128)(2,1)}), bf16[512,1280]{1,0:T(8,128)(2,1)}) %reduce-scatter.3.cloned.1.call-update) | async-done | bytes 1310736 | tf_op jit(solution)/shard_map/reduce_scatter | solution.py:113
  336.4 60.2 %all-gather.13.cloned.1.call-done = bf16[1280,2560]{1,0:T(8,128)(2,1)} async-done(((bf16[80,2560]{1,0:T(8,128)(2,1)}), bf16[1280,2560]{1,0:T(8,128)(2,1)}) %all-gather.13.cloned.1.call-update) | async-done | bytes 6553616 | tf_op jit(solution)/shard_map/all_gather | solution.py:138
  396.6 63.7 %all-gather.15.cloned.1.call-done = bf16[2560,1280]{0,1:T(8,128)(2,1)} async-done(((bf16[2560,80]{0,1:T(8,128)(2,1)}), bf16[2560,1280]{0,1:T(8,128)(2,1)}) %all-gather.15.cloned.1.call-update) | async-done | bytes 6553616 | tf_op jit(solution)/shard_map/all_gather | solution.py:142
  460.3 39.3 %all-gather.19.cloned.1.call-done = bf16[1024,1280]{1,0:T(8,128)(2,1)} async-done(((bf16[512,1280]{1,0:T(8,128)(2,1)}), bf16[1024,1280]{1,0:T(8,128)(2,1)}) %all-gather.19.cloned.1.call-update) | async-done | bytes 2621456 | tf_op jit(solution)/shard_map/all_gather | solution.py:131
  499.6 38.9 %fusion.58 = bf16[1024,1280]{1,0:T(8,128)(2,1)} fusion(bf16[2560,1280]{0,1:T(8,128)(2,1)} %all-gather.15.cloned.1.call-done, bf16[1024,1280]{1,0:T(8,128)(2,1)} %all-gather.19.cloned.1.call-done, bf16[1280,2560]{1,0:T(8,128)(2,1)} %all-gather.13.cloned.1.call-done), kind=kOutput, calls=%fused_computation.76 | convolution fusion | flops 13593477120 | bytes 18350080 | tf_op jit(solution)/shard_map/dot_general | solution.py:62
  538.5 37.8 %reduce-scatter.5.cloned.1.call-done = bf16[512,1280]{1,0:T(8,128)(2,1)} async-done(((bf16[1024,1280]{1,0:T(8,128)(2,1)}), bf16[512,1280]{1,0:T(8,128)(2,1)}) %reduce-scatter.5.cloned.1.call-update) | async-done | bytes 1310736 | tf_op jit(solution)/shard_map/reduce_scatter | solution.py:144
  576.4 3.1 fusion.104
  (81 shorter events, 62.6 us)
Async XLA Ops:
  6.5 110.9 %copy-start = (bf16[3,3,256,512]{3,2,1,0:T(8,128)(2,1)S(1)}, bf16[3,3,256,512]{3,2,1,0:T(8,128)(2,1)}, u32[]{:S(2)}) copy-start(bf16[3,3,256,512]{3,2,1,0:T(8,128)(2,1)} %param.20) | copy-start | bytes 7077892
  6.5 157.7 %all-gather.17.cloned.1.call-start = ((), (), s32[]{:S(2)}) async-start(), calls=%async_computation.8 | async-start | bytes 3932160 | tf_op jit(solution)/shard_map/all_gather | solution.py:103
  7.5 6.6 %collective-permute-start = (bf16[1,3,15,512]{3,2,1,0:T(8,128)(2,1)S(1)}, bf16[1,3,15,512]{3,2,1,0:T(8,128)(2,1)S(1)}, u32[]{:S(2)}, u32[]{:S(2)}) collective-permute-start(bf16[1,3,15,512]{3,2,1,0:T(8,128)(2,1)S(1)} %slice.12), channel_id=1, source_target_pairs={{0,1},{2,3},{4,5},{6,7},{8,9},{10,11},{12,13},{14,15},{16,17},{18,... | collective-permute-start | bytes 138248 | tf_op jit(solution)/shard_map/ppermute | solution.py:12
  18.8 21.0 %copy-start.6 = (bf16[3,3,3,64]{3,2,1,0:T(4,128)(2,1)S(1)}, bf16[3,3,3,64]{3,2,1,0:T(4,128)(2,1)}, u32[]{:S(2)}) copy-start(bf16[3,3,3,64]{3,2,1,0:T(4,128)(2,1)} %param.17) | copy-start | bytes 10372
  18.8 21.0 %copy-start.8 = (pred[8,33]{0,1:T(8,128)(4,1)S(1)}, pred[8,33]{0,1:T(8,128)(4,1)}, u32[]{:S(2)}) copy-start(pred[8,33]{0,1:T(8,128)(4,1)} %constant.128) | copy-start | bytes 796
  92.3 16.8 %copy-start.5 = (bf16[3,3,64,128]{3,2,1,0:T(8,128)(2,1)S(1)}, bf16[3,3,64,128]{3,2,1,0:T(8,128)(2,1)}, u32[]{:S(2)}) copy-start(bf16[3,3,64,128]{3,2,1,0:T(8,128)(2,1)} %param.18) | copy-start | bytes 442372
  109.1 6.7 %copy-start.4 = (bf16[3,3,128,256]{3,2,1,0:T(8,128)(2,1)S(1)}, bf16[3,3,128,256]{3,2,1,0:T(8,128)(2,1)}, u32[]{:S(2)}) copy-start(bf16[3,3,128,256]{3,2,1,0:T(8,128)(2,1)} %param.19) | copy-start | bytes 1769476
  123.0 97.6 %all-gather.9.cloned.1.call-start = ((), (), s32[]{:S(2)}) async-start(), calls=%async_computation.2 | async-start | bytes 5222400 | tf_op jit(solution)/shard_map/all_gather | solution.py:93
  123.7 165.7 %all-gather.11.cloned.1.call-start = ((), (), s32[]{:S(2)}) async-start(), calls=%async_computation.3 | async-start | bytes 1740800 | tf_op jit(solution)/shard_map/all_gather | solution.py:94
  124.5 207.1 %reduce-scatter.3.cloned.1.call-start = ((), (), s32[]{:S(2)}) async-start(), calls=%async_computation.4 | async-start | bytes 3932160 | tf_op jit(solution)/shard_map/reduce_scatter | solution.py:113
  169.0 59.8 %copy-start.7 = (f32[1280]{0:T(1024)S(1)}, f32[1280]{0:T(1024)}, u32[]{:S(2)}) copy-start(f32[1280]{0:T(1024)} %param.22) | copy-start | bytes 15364
  294.9 39.9 %copy-start.3 = (f32[1280]{0:T(1024)S(1)}, f32[1280]{0:T(1024)}, u32[]{:S(2)}) copy-start(f32[1280]{0:T(1024)} %param.25) | copy-start | bytes 15364
  295.0 101.6 %all-gather.13.cloned.1.call-start = ((), (), s32[]{:S(2)}) async-start(), calls=%async_computation.5 | async-start | bytes 6963200 | tf_op jit(solution)/shard_map/all_gather | solution.py:138
  295.5 164.8 %all-gather.15.cloned.1.call-start = ((), (), s32[]{:S(2)}) async-start(), calls=%async_computation.6 | async-start | bytes 6963200 | tf_op jit(solution)/shard_map/all_gather | solution.py:142
  296.1 203.5 %all-gather.19.cloned.1.call-start = ((), (), s32[]{:S(2)}) async-start(), calls=%async_computation.9 | async-start | bytes 3932160 | tf_op jit(solution)/shard_map/all_gather | solution.py:131
  333.7 1.1 copy-start.2
  336.3 240.1 %reduce-scatter.5.cloned.1.call-start = ((), (), s32[]{:S(2)}) async-start(), calls=%async_computation.7 | async-start | bytes 3932160 | tf_op jit(solution)/shard_map/reduce_scatter | solution.py:144
  499.6 79.8 %copy-start.1 = (bf16[3,3,256,512]{3,2,1,0:T(8,128)(2,1)S(1)}, bf16[3,3,256,512]{3,2,1,0:T(8,128)(2,1)}, u32[]{:S(2)}) copy-start(bf16[3,3,256,512]{3,2,1,0:T(8,128)(2,1)} %param.20) | copy-start | bytes 7077892
Sparse Core Ops, SparseCore 0:
  123.1 41.0 all-gather.16
  166.4 54.1 all-gather.8
  222.8 38.4 all-gather.10
  295.1 36.4 reduce-scatter.2
  333.7 62.8 all-gather.12
  398.7 61.5 all-gather.14
  461.9 37.7 all-gather.18
  538.7 37.6 reduce-scatter.4
where the time goes:
time: 598 us; the launch traced here: 587 us
  waiting for transfers between devices  332 us (56%)
  matrix products  130 us (22%)
  local copies, waits for them, and re-layouts  86.5 us (14%)
  other arithmetic  19.2 us (3%)
  between operations  14.1 us (2%)
    all_gather x1, waiting for transfers between devices, on_device(): down_part = lax.all_gather(down_weight, 'dp', axis=1, tiled=True)  63.7 us
    all_gather x1, waiting for transfers between devices, on_device(): lax.all_gather(up_weight, 'dp', axis=0, tiled=True)  60.2 us
    all_gather x1, waiting for transfers between devices, on_device(): lax.all_gather(qkv_weight, 'dp', axis=0, tiled=True)  51.6 us
    dot_general x2, matrix products, device_rows(): return jnp.dot(slab, weight, preferred_element_type=jnp.float32)  44.5 us
    convert_element_type x7, local copies, waits for them, and re-layouts, conv_rows(): return jax.nn.relu(out).astype(jnp.bfloat16)  41.8 us
    all_gather x1, waiting for transfers between devices, on_device(): lax.all_gather(tokens, 'space', axis=1, tiled=True)  39.7 us
    all_gather x1, waiting for transfers between devices, on_device(): group_rows = lax.all_gather(normed_two, 'space', axis=1, tiled=True)  39.3 us
    reduce_scatter x1, waiting for transfers between devices, on_device(): lax.psum_scatter(device_rows(hidden, jnp.int32(0), groups * count * lax.a...  37.8 us
  transfers between devices with their start and end apart: 9, of which 8 were waited for; matrix products, arithmetic and copies ran while one was open for 13% of the time, Pallas kernels for 0%

commit v1 on v0

--- a/solution.py
+++ b/solution.py
@@ -139,7 +139,21 @@
         preferred_element_type=jnp.float32,
     )
     hidden = jax.nn.gelu(before_gelu, approximate=False).astype(jnp.bfloat16)
-    down_part = lax.all_gather(down_weight, "dp", axis=1, tiled=True)
+
+    def bind_state_on_mesh(mat):
+        num_devices = lax.axis_size("dp")
+        tray = [mat]
+        for to_i in range(num_devices - 1):
+            tray.append(
+                lax.ppermute(
+                    tray[-1], "dp", [(at, (at + 1) % num_devices) for at in range(num_devices)]
+                )
+            )
+        return jnp.roll(
+            jnp.concatenate(tray[::-1], axis=1), (lax.axis_index("dp") + 1) * mat.shape[1], axis=1
+        )
+
+    down_part = bind_state_on_mesh(down_weight)
     mlp_sum = (
         lax.psum_scatter(
             device_rows(

time: 598 us -> 660 us (1.10)
  local copies, waits for them, and re-layouts: 86.5 us -> 133 us
  matrix products: 130 us -> 142 us
    ppermute x0 -> x15, waiting for transfers between devices: none -> 176 us  [bind_state_on_mesh(): lax.ppermute(tray[-1], 'dp', [(at, (at + 1) % num_devices) for at in rang...]
    all_gather x1 -> x0, waiting for transfers between devices: 63.7 us -> none  [on_device(): down_part = lax.all_gather(down_weight, 'dp', axis=1, tiled=True)]
    all_gather x1, waiting for transfers between devices: 60.2 us -> 0.01 us  [on_device(): lax.all_gather(up_weight, 'dp', axis=0, tiled=True)]
    unnamed x18 -> x75, local copies, waits for them, and re-layouts: 0.6 us -> 46.1 us
    reduce_scatter x1, waiting for transfers between devices: 35.4 us -> 0.01 us  [on_device(): lax.psum_scatter(device_rows(mixed, jnp.int32(0), groups * count * lax.ax...]
    all_gather x1, waiting for transfers between devices: 39.3 us -> 25.9 us  [on_device(): group_rows = lax.all_gather(normed_two, 'space', axis=1, tiled=True)]
    conv_general_dilated x4, matrix products: 37.5 us -> 49.4 us  [conv_rows(): lax.conv_general_dilated(image_field, kernel, (2, 2), ((0, 0), (1, 1)), d...]
  transfers between devices with their start and end apart: 9 -> 23, of which waited for: 8 -> 20; matrix products, arithmetic and copies ran while one was open for 13% -> 19% of each run, Pallas kernels for 0% -> 0%
where the time goes in v1:
time: 660 us; the launch traced here: 648 us
  waiting for transfers between devices  334 us (51%)
  matrix products  142 us (22%)
  local copies, waits for them, and re-layouts  133 us (20%)
  other arithmetic  19.2 us (3%)
  between operations  14.1 us (2%)
    ppermute x15, waiting for transfers between devices, bind_state_on_mesh(): lax.ppermute(tray[-1], 'dp', [(at, (at + 1) % num_devices) for at in rang...  176 us
    all_gather x1, waiting for transfers between devices, on_device(): lax.all_gather(qkv_weight, 'dp', axis=0, tiled=True)  51.6 us
    conv_general_dilated x4, matrix products, conv_rows(): lax.conv_general_dilated(image_field, kernel, (2, 2), ((0, 0), (1, 1)), d...  49.4 us
    unnamed x75, local copies, waits for them, and re-layouts  46.1 us
    dot_general x2, matrix products, device_rows(): return jnp.dot(slab, weight, preferred_element_type=jnp.float32)  45.2 us
    convert_element_type x7, local copies, waits for them, and re-layouts, conv_rows(): return jax.nn.relu(out).astype(jnp.bfloat16)  41.9 us
    all_gather x1, waiting for transfers between devices, on_device(): lax.all_gather(tokens, 'space', axis=1, tiled=True)  39.7 us
    reduce_scatter x1, waiting for transfers between devices, on_device(): lax.psum_scatter(device_rows(hidden, jnp.int32(0), groups * count * lax.a...  37.8 us
  transfers between devices with their start and end apart: 23, of which 20 were waited for; matrix products, arithmetic and copies ran while one was open for 19% of the time, Pallas kernels for 0%

profile of v1, /device:TPU:0, one launch (start us, length us, event | category | flops | bytes accessed | tf_op | source)
XLA Modules:
  0.0 648.1 jit_solution(9700133494078263349)
XLA Ops:
  18.8 19.6 %copy.46 = bf16[3,271,1,8,66]{3,0,4,1,2:T(4,128)(2,1)} copy(bf16[3,271,1,8,66]{4,3,1,0,2:T(8,128)(2,1)} %reshape.228) | data formatting | bytes 1717056 | tf_op jit(solution)/shard_map/conv_general_dilated | solution.py:16
  39.9 27.8 %fusion.44 = bf16[135,8,33,64]{3,1,2,0:T(8,128)(2,1)} fusion(pred[8,33]{0,1:T(8,128)(4,1)S(1)} %copy-done.21, bf16[3,3,3,64]{3,2,1,0:T(4,128)(2,1)S(1)} %copy-done.19, bf16[3,271,1,7,2]{3,0,4,1,2:T(4,128)(2,1)S(1)} %slice.25, bf16[3,271,1,8,66]{3,0,4,1,2:T(4,128)(2,1)} %copy.46), kind=kOutput, calls=%fused_computation.57 | convolution fusion | flops 134949312 | bytes 5446932 | tf_op jit(solution)/shard_map/conv_general_dilated | solution.py:16
  67.7 16.4 %copy.47 = bf16[135,8,33,64]{0,3,2,1:T(8,128)(2,1)} copy(bf16[135,8,33,64]{3,1,2,0:T(8,128)(2,1)} %fusion.44) | data formatting | bytes 9123840 | tf_op jit(solution)/shard_map/convert_element_type | solution.py:24
  92.4 15.6 %copy.48 = bf16[135,1,8,32,64]{4,2,3,0,1:T(8,128)(2,1)} copy(bf16[135,1,8,32,64]{0,4,3,2,1:T(8,128)(2,1)} %bitcast.114) | data formatting | bytes 8847360 | tf_op jit(solution)/shard_map/convert_element_type | solution.py:24
  109.2 18.6 %fusion.118 = bf16[67,1,8,16,128]{4,2,3,0,1:T(8,128)(2,1)S(1)} fusion(bf16[3,3,64,128]{3,2,1,0:T(8,128)(2,1)S(1)} %copy-done.18, bf16[135,1,7,1,64]{4,2,3,0,1:T(8,128)(2,1)S(1)} %get-tuple-element.63, bf16[135,1,7,1,64]{4,2,3,0,1:T(8,128)(2,1)S(1)} %get-tuple-element.62, bf16[135,1,8,32,64]{4,2,3,0,1:T(8,128)(2,1)} %copy.48), kind=kOutput, calls=%fused_computation.135 | convolution fusion | flops 1290278912 | bytes 7008512 | tf_op jit(solution)/shard_map/conv_general_dilated | solution.py:16
  136.6 39.7 %all-gather.14.cloned.1.call-done = bf16[1024,1280]{1,0:T(8,128)(2,1)} async-done(((bf16[512,1280]{1,0:T(8,128)(2,1)}), bf16[1024,1280]{1,0:T(8,128)(2,1)}) %all-gather.14.cloned.1.call-update) | async-done | bytes 2621456 | tf_op jit(solution)/shard_map/all_gather | solution.py:103
  181.0 51.6 %all-gather.8.cloned.1.call-done = bf16[1280,3,640]{2,0,1:T(8,128)(2,1)} async-done(((bf16[80,3,640]{2,0,1:T(8,128)(2,1)}), bf16[1280,3,640]{2,0,1:T(8,128)(2,1)}) %all-gather.8.cloned.1.call-update) | async-done | bytes 4915216 | tf_op jit(solution)/shard_map/all_gather | solution.py:93
  240.8 10.4 %convolution_convert_fusion.1 = bf16[1024,1920]{1,0:T(8,128)(2,1)} fusion(bf16[1280,1920]{0,1:T(8,128)(2,1)} %bitcast.116, bf16[1024,1280]{1,0:T(8,128)(2,1)} %all-gather.14.cloned.1.call-done, f32[1280]{0:T(1024)S(1)} %copy-done.20, f32[1024]{0:T(1024)S(1)} %add_rsqrt_fusion, f32[1024]{0:T(1024)S(1)} %broadcast_multiply_fusion), kind=kOutput, calls=%fused_computation.108 | convolution fusion | flops 5041684480 | bytes 11482112 | tf_op jit(solution)/shard_map/dot_general | solution.py:102
  261.7 39.8 %while.10 = (s32[]{:T(128)}, bf16[8,1,1024,80]{2,3,1,0:T(8,128)(2,1)}, bf16[8,1,1024,80]{2,3,0,1:T(8,128)(2,1)}, bf16[8,1,1024,80]{2,3,0,1:T(8,128)(2,1)S(1)}, bf16[8,1,1024,80]{2,3,0,1:T(8,128)(2,1)}, /*index=5*/s32[]{:T(128)}) while((s32[]{:T(128)}, bf16[8,1,1024,80]{2,3,1,0:T(8,128)(2,1)}, bf16[8,1,1024,80]{2,3,0,1:T(8,128)(2,1)}, ...), condition=%wide.region_5.6_spmd, body=%wide.region_2.5_spmd.sunk | while | flops 345061376 | bytes 13260869 | solution.py:49
  317.4 10.1 %collective-permute-done.2 = bf16[2560,80]{0,1:T(8,128)(2,1)S(1)} collective-permute-done((bf16[2560,80]{0,1:T(8,128)(2,1)S(1)}, bf16[2560,80]{0,1:T(8,128)(2,1)S(1)}, u32[]{:S(2)}, u32[]{:S(2)}) %collective-permute-start.2) | collective-permute-done | bytes 409632 | tf_op jit(solution)/shard_map/ppermute | solution.py:148
  327.5 10.1 %collective-permute-done.3 = bf16[2560,80]{0,1:T(8,128)(2,1)S(1)} collective-permute-done((bf16[2560,80]{0,1:T(8,128)(2,1)S(1)}, bf16[2560,80]{0,1:T(8,128)(2,1)S(1)}, u32[]{:S(2)}, u32[]{:S(2)}) %collective-permute-start.3) | collective-permute-done | bytes 409632 | tf_op jit(solution)/shard_map/ppermute | solution.py:148
  337.5 10.1 %collective-permute-done.4 = bf16[2560,80]{0,1:T(8,128)(2,1)S(1)} collective-permute-done((bf16[2560,80]{0,1:T(8,128)(2,1)S(1)}, bf16[2560,80]{0,1:T(8,128)(2,1)S(1)}, u32[]{:S(2)}, u32[]{:S(2)}) %collective-permute-start.4) | collective-permute-done | bytes 409632 | tf_op jit(solution)/shard_map/ppermute | solution.py:148
  347.6 10.1 %collective-permute-done.5 = bf16[2560,80]{0,1:T(8,128)(2,1)S(1)} collective-permute-done((bf16[2560,80]{0,1:T(8,128)(2,1)S(1)}, bf16[2560,80]{0,1:T(8,128)(2,1)S(1)}, u32[]{:S(2)}, u32[]{:S(2)}) %collective-permute-start.5) | collective-permute-done | bytes 409632 | tf_op jit(solution)/shard_map/ppermute | solution.py:148
  357.7 10.1 %collective-permute-done.6 = bf16[2560,80]{0,1:T(8,128)(2,1)S(1)} collective-permute-done((bf16[2560,80]{0,1:T(8,128)(2,1)S(1)}, bf16[2560,80]{0,1:T(8,128)(2,1)S(1)}, u32[]{:S(2)}, u32[]{:S(2)}) %collective-permute-start.6) | collective-permute-done | bytes 409632 | tf_op jit(solution)/shard_map/ppermute | solution.py:148
  389.5 10.2 %collective-permute-done.9 = bf16[2560,80]{0,1:T(8,128)(2,1)} collective-permute-done((bf16[2560,80]{0,1:T(8,128)(2,1)S(1)}, bf16[2560,80]{0,1:T(8,128)(2,1)}, u32[]{:S(2)}, u32[]{:S(2)}) %collective-permute-start.9) | collective-permute-done | bytes 409632 | tf_op jit(solution)/shard_map/ppermute | solution.py:148
  399.7 10.3 %collective-permute-done.10 = bf16[2560,80]{0,1:T(8,128)(2,1)} collective-permute-done((bf16[2560,80]{0,1:T(8,128)(2,1)}, bf16[2560,80]{0,1:T(8,128)(2,1)}, u32[]{:S(2)}, u32[]{:S(2)}) %collective-permute-start.10) | collective-permute-done | bytes 409632 | tf_op jit(solution)/shard_map/ppermute | solution.py:148
  410.0 19.0 %collective-permute-done.11 = bf16[2560,80]{0,1:T(8,128)(2,1)S(1)} collective-permute-done((bf16[2560,80]{0,1:T(8,128)(2,1)}, bf16[2560,80]{0,1:T(8,128)(2,1)S(1)}, u32[]{:S(2)}, u32[]{:S(2)}) %collective-permute-start.11) | collective-permute-done | bytes 409632 | tf_op jit(solution)/shard_map/ppermute | solution.py:148
  429.8 10.2 %collective-permute-done.12 = bf16[2560,80]{0,1:T(8,128)(2,1)S(1)} collective-permute-done((bf16[2560,80]{0,1:T(8,128)(2,1)S(1)}, bf16[2560,80]{0,1:T(8,128)(2,1)S(1)}, u32[]{:S(2)}, u32[]{:S(2)}) %collective-permute-start.12) | collective-permute-done | bytes 409632 | tf_op jit(solution)/shard_map/ppermute | solution.py:148
  440.8 19.0 %collective-permute-done.13 = bf16[2560,80]{0,1:T(8,128)(2,1)S(1)} collective-permute-done((bf16[2560,80]{0,1:T(8,128)(2,1)S(1)}, bf16[2560,80]{0,1:T(8,128)(2,1)S(1)}, u32[]{:S(2)}, u32[]{:S(2)}) %collective-permute-start.13) | collective-permute-done | bytes 409632 | tf_op jit(solution)/shard_map/ppermute | solution.py:148
  460.5 16.3 %collective-permute-done.14 = bf16[2560,80]{0,1:T(8,128)(2,1)} collective-permute-done((bf16[2560,80]{0,1:T(8,128)(2,1)S(1)}, bf16[2560,80]{0,1:T(8,128)(2,1)}, u32[]{:S(2)}, u32[]{:S(2)}) %collective-permute-start.14) | collective-permute-done | bytes 409632 | tf_op jit(solution)/shard_map/ppermute | solution.py:148
  476.8 10.4 %collective-permute-done.15 = bf16[2560,80]{0,1:T(8,128)(2,1)} collective-permute-done((bf16[2560,80]{0,1:T(8,128)(2,1)}, bf16[2560,80]{0,1:T(8,128)(2,1)}, u32[]{:S(2)}, u32[]{:S(2)}) %collective-permute-start.15) | collective-permute-done | bytes 409632 | tf_op jit(solution)/shard_map/ppermute | solution.py:148
  534.5 25.9 %all-gather.16.cloned.1.call-done = bf16[1024,1280]{1,0:T(8,128)(2,1)} async-done(((bf16[512,1280]{1,0:T(8,128)(2,1)}), bf16[1024,1280]{1,0:T(8,128)(2,1)}) %all-gather.16.cloned.1.call-update) | async-done | bytes 2621456 | tf_op jit(solution)/shard_map/all_gather | solution.py:131
  560.4 39.5 %fusion.88 = bf16[1024,1280]{1,0:T(8,128)(2,1)} fusion(bf16[2560,2560]{0,1:T(8,128)(2,1)} %constant_dynamic-update-slice_fusion, s32[]{:T(128)S(6)} %select_n.19, bf16[1024,1280]{1,0:T(8,128)(2,1)} %all-gather.16.cloned.1.call-done, bf16[1280,2560]{1,0:T(8,128)(2,1)} %all-gather.12.cloned.1.call-done), kind=kOutput, calls=%fused_computation.106 | convolution fusion | flops 13593477120 | bytes 18350084 | tf_op jit(solution)/shard_map/dot_general | solution.py:62
  600.0 37.8 %reduce-scatter.5.cloned.1.call-done = bf16[512,1280]{1,0:T(8,128)(2,1)} async-done(((bf16[1024,1280]{1,0:T(8,128)(2,1)}), bf16[512,1280]{1,0:T(8,128)(2,1)}) %reduce-scatter.5.cloned.1.call-update) | async-done | bytes 1310736 | tf_op jit(solution)/shard_map/reduce_scatter | solution.py:158
  (166 shorter events, 185.3 us)
Async XLA Ops:
  6.5 169.7 %all-gather.14.cloned.1.call-start = ((), (), s32[]{:S(2)}) async-start(), calls=%async_computation.7 | async-start | bytes 3932160 | tf_op jit(solution)/shard_map/all_gather | solution.py:103
  7.5 6.6 %collective-permute-start = (bf16[1,3,15,512]{3,2,1,0:T(8,128)(2,1)S(1)}, bf16[1,3,15,512]{3,2,1,0:T(8,128)(2,1)S(1)}, u32[]{:S(2)}, u32[]{:S(2)}) collective-permute-start(bf16[1,3,15,512]{3,2,1,0:T(8,128)(2,1)S(1)} %slice.12), channel_id=1, source_target_pairs={{0,1},{2,3},{4,5},{6,7},{8,9},{10,11},{12,13},{14,15},{16,17},{18,... | collective-permute-start | bytes 138248 | tf_op jit(solution)/shard_map/ppermute | solution.py:12
  135.0 97.6 %all-gather.8.cloned.1.call-start = ((), (), s32[]{:S(2)}) async-start(), calls=%async_computation.2 | async-start | bytes 5222400 | tf_op jit(solution)/shard_map/all_gather | solution.py:93
  135.8 165.8 %all-gather.10.cloned.1.call-start = ((), (), s32[]{:S(2)}) async-start(), calls=%async_computation.3 | async-start | bytes 1740800 | tf_op jit(solution)/shard_map/all_gather | solution.py:94
  136.5 382.7 %reduce-scatter.3.cloned.1.call-start = ((), (), s32[]{:S(2)}) async-start(), calls=%async_computation.4 | async-start | bytes 3932160 | tf_op jit(solution)/shard_map/reduce_scatter | solution.py:113
  307.2 227.3 %all-gather.12.cloned.1.call-start = ((), (), s32[]{:S(2)}) async-start(), calls=%async_computation.5 | async-start | bytes 6963200 | tf_op jit(solution)/shard_map/all_gather | solution.py:138
  307.3 10.1 %collective-permute-start.1 = (bf16[2560,80]{0,1:T(8,128)(2,1)S(1)}, bf16[2560,80]{0,1:T(8,128)(2,1)S(1)}, u32[]{:S(2)}, u32[]{:S(2)}) collective-permute-start(bf16[2560,80]{0,1:T(8,128)(2,1)S(1)} %copy-done.3), channel_id=1, source_target_pairs={{0,2},{2,4},{4,6},{6,8},{8,10},{10,12},{12,14},{14,16},{16,18},{18... | collective-permute-start | bytes 1228808 | tf_op jit(solution)/shard_map/ppermute | solution.py:148
  317.4 10.1 %collective-permute-start.2 = (bf16[2560,80]{0,1:T(8,128)(2,1)S(1)}, bf16[2560,80]{0,1:T(8,128)(2,1)S(1)}, u32[]{:S(2)}, u32[]{:S(2)}) collective-permute-start(bf16[2560,80]{0,1:T(8,128)(2,1)S(1)} %collective-permute-done.1), channel_id=1, source_target_pairs={{0,2},{2,4},{4,6},{6,8},{8,10},{10,12},{12,14},{14,16},{16,18},{18... | collective-permute-start | bytes 1228808 | tf_op jit(solution)/shard_map/ppermute | solution.py:148
  327.5 10.1 %collective-permute-start.3 = (bf16[2560,80]{0,1:T(8,128)(2,1)S(1)}, bf16[2560,80]{0,1:T(8,128)(2,1)S(1)}, u32[]{:S(2)}, u32[]{:S(2)}) collective-permute-start(bf16[2560,80]{0,1:T(8,128)(2,1)S(1)} %collective-permute-done.2), channel_id=1, source_target_pairs={{0,2},{2,4},{4,6},{6,8},{8,10},{10,12},{12,14},{14,16},{16,18},{18... | collective-permute-start | bytes 1228808 | tf_op jit(solution)/shard_map/ppermute | solution.py:148
  337.5 10.1 %collective-permute-start.4 = (bf16[2560,80]{0,1:T(8,128)(2,1)S(1)}, bf16[2560,80]{0,1:T(8,128)(2,1)S(1)}, u32[]{:S(2)}, u32[]{:S(2)}) collective-permute-start(bf16[2560,80]{0,1:T(8,128)(2,1)S(1)} %collective-permute-done.3), channel_id=1, source_target_pairs={{0,2},{2,4},{4,6},{6,8},{8,10},{10,12},{12,14},{14,16},{16,18},{18... | collective-permute-start | bytes 1228808 | tf_op jit(solution)/shard_map/ppermute | solution.py:148
  347.6 170.8 %copy-start.4 = (bf16[2560,80]{0,1:T(8,128)(2,1)}, bf16[2560,80]{0,1:T(8,128)(2,1)S(1)}, u32[]{:S(2)}) copy-start(bf16[2560,80]{0,1:T(8,128)(2,1)S(1)} %collective-permute-done.4) | copy-start | bytes 1228804
  347.6 10.1 %collective-permute-start.5 = (bf16[2560,80]{0,1:T(8,128)(2,1)S(1)}, bf16[2560,80]{0,1:T(8,128)(2,1)S(1)}, u32[]{:S(2)}, u32[]{:S(2)}) collective-permute-start(bf16[2560,80]{0,1:T(8,128)(2,1)S(1)} %collective-permute-done.4), channel_id=1, source_target_pairs={{0,2},{2,4},{4,6},{6,8},{8,10},{10,12},{12,14},{14,16},{16,18},{18... | collective-permute-start | bytes 1228808 | tf_op jit(solution)/shard_map/ppermute | solution.py:148
  357.7 10.1 %collective-permute-start.6 = (bf16[2560,80]{0,1:T(8,128)(2,1)S(1)}, bf16[2560,80]{0,1:T(8,128)(2,1)S(1)}, u32[]{:S(2)}, u32[]{:S(2)}) collective-permute-start(bf16[2560,80]{0,1:T(8,128)(2,1)S(1)} %collective-permute-done.5), channel_id=1, source_target_pairs={{0,2},{2,4},{4,6},{6,8},{8,10},{10,12},{12,14},{14,16},{16,18},{18... | collective-permute-start | bytes 1228808 | tf_op jit(solution)/shard_map/ppermute | solution.py:148
  367.8 10.1 %collective-permute-start.7 = (bf16[2560,80]{0,1:T(8,128)(2,1)S(1)}, bf16[2560,80]{0,1:T(8,128)(2,1)S(1)}, u32[]{:S(2)}, u32[]{:S(2)}) collective-permute-start(bf16[2560,80]{0,1:T(8,128)(2,1)S(1)} %collective-permute-done.6), channel_id=1, source_target_pairs={{0,2},{2,4},{4,6},{6,8},{8,10},{10,12},{12,14},{14,16},{16,18},{18... | collective-permute-start | bytes 1228808 | tf_op jit(solution)/shard_map/ppermute | solution.py:148
  378.6 10.1 %collective-permute-start.8 = (bf16[2560,80]{0,1:T(8,128)(2,1)S(1)}, bf16[2560,80]{0,1:T(8,128)(2,1)S(1)}, u32[]{:S(2)}, u32[]{:S(2)}) collective-permute-start(bf16[2560,80]{0,1:T(8,128)(2,1)S(1)} %collective-permute-done.7), channel_id=1, source_target_pairs={{0,2},{2,4},{4,6},{6,8},{8,10},{10,12},{12,14},{14,16},{16,18},{18... | collective-permute-start | bytes 1228808 | tf_op jit(solution)/shard_map/ppermute | solution.py:148
  389.5 10.2 %collective-permute-start.9 = (bf16[2560,80]{0,1:T(8,128)(2,1)S(1)}, bf16[2560,80]{0,1:T(8,128)(2,1)}, u32[]{:S(2)}, u32[]{:S(2)}) collective-permute-start(bf16[2560,80]{0,1:T(8,128)(2,1)S(1)} %collective-permute-done.8), channel_id=1, source_target_pairs={{0,2},{2,4},{4,6},{6,8},{8,10},{10,12},{12,14},{14,16},{16,18},{18... | collective-permute-start | bytes 1228808 | tf_op jit(solution)/shard_map/ppermute | solution.py:148
  399.6 10.4 %collective-permute-start.10 = (bf16[2560,80]{0,1:T(8,128)(2,1)}, bf16[2560,80]{0,1:T(8,128)(2,1)}, u32[]{:S(2)}, u32[]{:S(2)}) collective-permute-start(bf16[2560,80]{0,1:T(8,128)(2,1)} %collective-permute-done.9), channel_id=1, source_target_pairs={{0,2},{2,4},{4,6},{6,8},{8,10},{10,12},{12,14},{14,16},{16,18},{18... | collective-permute-start | bytes 1228808 | tf_op jit(solution)/shard_map/ppermute | solution.py:148
  399.7 160.7 %all-gather.16.cloned.1.call-start = ((), (), s32[]{:S(2)}) async-start(), calls=%async_computation.8 | async-start | bytes 3932160 | tf_op jit(solution)/shard_map/all_gather | solution.py:131
  410.0 19.0 %collective-permute-start.11 = (bf16[2560,80]{0,1:T(8,128)(2,1)}, bf16[2560,80]{0,1:T(8,128)(2,1)S(1)}, u32[]{:S(2)}, u32[]{:S(2)}) collective-permute-start(bf16[2560,80]{0,1:T(8,128)(2,1)} %collective-permute-done.10), channel_id=1, source_target_pairs={{0,2},{2,4},{4,6},{6,8},{8,10},{10,12},{12,14},{14,16},{16,18},{18... | collective-permute-start | bytes 1228808 | tf_op jit(solution)/shard_map/ppermute | solution.py:148
  429.8 10.2 %collective-permute-start.12 = (bf16[2560,80]{0,1:T(8,128)(2,1)S(1)}, bf16[2560,80]{0,1:T(8,128)(2,1)S(1)}, u32[]{:S(2)}, u32[]{:S(2)}) collective-permute-start(bf16[2560,80]{0,1:T(8,128)(2,1)S(1)} %collective-permute-done.11), channel_id=1, source_target_pairs={{0,2},{2,4},{4,6},{6,8},{8,10},{10,12},{12,14},{14,16},{16,18},{18... | collective-permute-start | bytes 1228808 | tf_op jit(solution)/shard_map/ppermute | solution.py:148
  440.8 19.0 %collective-permute-start.13 = (bf16[2560,80]{0,1:T(8,128)(2,1)S(1)}, bf16[2560,80]{0,1:T(8,128)(2,1)S(1)}, u32[]{:S(2)}, u32[]{:S(2)}) collective-permute-start(bf16[2560,80]{0,1:T(8,128)(2,1)S(1)} %collective-permute-done.12), channel_id=1, source_target_pairs={{0,2},{2,4},{4,6},{6,8},{8,10},{10,12},{12,14},{14,16},{16,18},{18... | collective-permute-start | bytes 1228808 | tf_op jit(solution)/shard_map/ppermute | solution.py:148
  460.5 16.3 %collective-permute-start.14 = (bf16[2560,80]{0,1:T(8,128)(2,1)S(1)}, bf16[2560,80]{0,1:T(8,128)(2,1)}, u32[]{:S(2)}, u32[]{:S(2)}) collective-permute-start(bf16[2560,80]{0,1:T(8,128)(2,1)S(1)} %collective-permute-done.13), channel_id=1, source_target_pairs={{0,2},{2,4},{4,6},{6,8},{8,10},{10,12},{12,14},{14,16},{16,18},{18... | collective-permute-start | bytes 1228808 | tf_op jit(solution)/shard_map/ppermute | solution.py:148
  476.8 10.4 %collective-permute-start.15 = (bf16[2560,80]{0,1:T(8,128)(2,1)}, bf16[2560,80]{0,1:T(8,128)(2,1)}, u32[]{:S(2)}, u32[]{:S(2)}) collective-permute-start(bf16[2560,80]{0,1:T(8,128)(2,1)} %collective-permute-done.14), channel_id=1, source_target_pairs={{0,2},{2,4},{4,6},{6,8},{8,10},{10,12},{12,14},{14,16},{16,18},{18... | collective-permute-start | bytes 1228808 | tf_op jit(solution)/shard_map/ppermute | solution.py:148
  524.0 113.8 %reduce-scatter.5.cloned.1.call-start = ((), (), s32[]{:S(2)}) async-start(), calls=%async_computation.6 | async-start | bytes 3932160 | tf_op jit(solution)/shard_map/reduce_scatter | solution.py:158
  (21 other events, 882.6 us)
Sparse Core Ops, SparseCore 0:
  135.1 41.0 all-gather.13
  178.5 54.1 all-gather.7
  234.8 38.4 all-gather.9
  307.3 36.3 reduce-scatter.2
  399.8 72.4 all-gather.11
  524.2 36.2 all-gather.15
  600.1 37.6 reduce-scatter.4
